TPU v7x, 32 devices: a whole 2x2x4 slice. The times are simulated.
32 devices in a mesh: row: 4 (over x, core), col: 8 (over z, y).
Axes of the slice: x: 2, y: 2, z: 4, core: 2. Of those that a mesh axis runs over, the one named last changes fastest.
Arguments:
- tensor: float32 [1024, 32, 1024], P(None, 'row', 'col'), may hold values from -60 to 60, as said below
- factor_two: float32 [32, 32], P('row'), may hold values from -1 to 1
- factor_three: float32 [32, 32], P('col'), may hold values from -1 to 1
- factor_four: float32 [32, 16], replicated, may hold values from -1 to 1
- factor_init: float32 [1024, 64], replicated, may hold values from -6 to 6
Outputs:
- factor_new: float32 [1024, 64], replicated
- core: float32 [64, 32, 32, 16], P(None, 'row', 'col')
Inputs may be any that keep to these rules, and one draw needn't show every extreme that they name: `tensor`: scales vary from slab to slab.
All inputs are finite; a program needn't handle non-finite values.
Results may differ from a plain program's by a relative error of at most 0.00013.
Values sent between devices are 32-bit elements; how exact they have to be, the bound alone decides.
A program may use at most 128 MiB of HBM per device.

v0:
```python
import jax
import jax.numpy as jnp
from jax import lax
from jax.sharding import PartitionSpec as P


def shards(tensor, factor_two, factor_three, factor_four, factor_init):
    highest = lax.Precision.HIGHEST
    first_len = tensor.shape[0]
    local_two = tensor.shape[1]
    fourth_len = factor_four.shape[0]
    local_three = tensor.shape[2] // fourth_len
    rank_one = factor_init.shape[1]
    data = tensor.reshape(first_len, local_two, local_three, fourth_len)
    fourth = jnp.einsum("abcd,de->abce", data, factor_four, precision=highest)
    whole_two = lax.all_gather(factor_two, "row", axis=0, tiled=True)
    spread_two = lax.all_to_all(fourth, "row", split_axis=0, concat_axis=1, tiled=True)
    projected_two = jnp.einsum("abce,bg->agce", spread_two, whole_two, precision=highest)
    partial_two = lax.all_to_all(projected_two, "row", split_axis=1, concat_axis=0, tiled=True)
    whole_three = lax.all_gather(factor_three, "col", axis=0, tiled=True)
    spread_three = lax.all_to_all(partial_two, "col", split_axis=0, concat_axis=2, tiled=True)
    projected_three = jnp.einsum("agce,cf->agfe", spread_three, whole_three, precision=highest)
    block = lax.all_to_all(projected_three, "col", split_axis=2, concat_axis=0, tiled=True)
    columns = block.reshape(first_len, -1)
    basis = factor_init
    local_gram = jnp.dot(columns, columns.T, precision=highest, preferred_element_type=jnp.float32)
    gram = lax.psum(local_gram, ("row", "col"))
    image = jnp.dot(gram, basis, precision=highest, preferred_element_type=jnp.float32)
    square = jnp.dot(image.T, image, precision=highest, preferred_element_type=jnp.float32)
    lower = jnp.linalg.cholesky(square)
    basis = jax.scipy.linalg.solve_triangular(lower, image.T, lower=True).T
    core = jnp.dot(basis.T, columns, precision=highest, preferred_element_type=jnp.float32)
    return (basis, core.reshape(rank_one, block.shape[1], block.shape[2], block.shape[3]))


def solution(mesh):
    in_specs = (P(None, "row", "col"), P("row", None), P("col", None), P(), P())
    out_specs = (P(), P(None, "row", "col", None))
    return jax.shard_map(shards, mesh=mesh, in_specs=in_specs, out_specs=out_specs, check_vma=False)
```

profile of v0, /device:TPU:0, one launch (start us, length us, event | category | flops | bytes accessed | tf_op | source)
XLA Modules:
  0.0 512.5 jit_solution(1816454857235836736)
XLA Ops:
  7.2 5.5 %copy.18 = f32[1024,8,128]{0,2,1:T(8,128)} copy(f32[1024,8,128]{2,1,0:T(8,128)} %param.5) | data formatting | bytes 8388608 | tf_op args[0]
  12.6 4.2 fusion.12
  16.8 12.2 %copy.19 = f32[1024,8,4,16]{3,2,1,0:T(4,128)} copy(f32[1024,8,4,16]{0,3,2,1:T(8,128)S(1)} %fusion.12) | data formatting | bytes 4194304 | tf_op jit(solution)/shard_map/abcd,de->abce/dot_general | solution.py:15
  29.0 15.5 %reshape.31 = f32[4,1,131072]{2,1,0:T(1,128)} reshape(f32[1024,8,4,16]{3,2,1,0:T(4,128)} %copy.19) | data formatting | bytes 4194304
  44.5 4.4 all-to-all-start
  48.9 26.7 %all_gather.6 = f32[32,32]{1,0:T(8,128)S(1)} all-gather(f32[8,32]{1,0:T(8,128)S(1)} %copy-done.5), channel_id=1, replica_groups=mesh['row'=4,'col'=8] {'row'}, dimensions={0}, use_global_device_ids=true | all-gather | bytes 5120 | tf_op jit(solution)/shard_map/all_gather | solution.py:16
  75.5 1.4 copy-done.2
  77.4 7.7 %reduce.6 = f32[4,131072]{1,0:T(4,128)S(1)} reduce(f32[4,1,131072]{2,1,0:T(1,128)} %copy-done.2, f32[]{:T(128)} %broadcast.53), dimensions={1}, to_apply=%all_to_all.50.reduce_sub_computation | reduce | bytes 4194308 | tf_op jit(solution)/shard_map/all_to_all | solution.py:17
  85.1 17.9 %reshape.32 = f32[1024,8,4,16]{3,2,1,0:T(4,128)} reshape(f32[4,131072]{1,0:T(4,128)S(1)} %reduce.6) | data formatting | bytes 4194304
  103.0 12.2 %copy.20 = f32[4,256,8,4,16]{1,2,0,4,3:T(8,128)S(1)} copy(f32[4,256,8,4,16]{4,3,2,1,0:T(4,128)} %bitcast.72) | data formatting | bytes 4194304 | tf_op jit(solution)/shard_map/all_to_all | solution.py:17
  115.3 1.9 fusion.2
  117.2 1.2 copy.21
  118.4 28.1 %all_to_all.69 = f32[256,32,4,16]{0,3,2,1:T(8,128)S(1)} all-to-all(f32[256,32,4,16]{0,3,2,1:T(8,128)S(1)} %copy.21), channel_id=1, replica_groups=mesh['row'=4,'col'=8] {'row'}, dimensions={1} | all-to-all | bytes 4194304 | tf_op jit(solution)/shard_map/all_to_all | solution.py:19
  146.6 12.1 %copy.37 = f32[256,4,8,4,16]{4,3,2,0,1:T(4,128)} copy(f32[256,4,8,4,16]{0,4,3,2,1:T(8,128)S(1)} %bitcast.78) | data formatting | bytes 4194304 | tf_op jit(solution)/shard_map/all_to_all | solution.py:19
  158.6 15.4 %reshape.33 = f32[8,1,65536]{2,1,0:T(1,128)} reshape(f32[1024,8,4,16]{3,2,1,0:T(4,128)} %bitcast.73) | data formatting | bytes 4194304
  174.0 6.8 %all-to-all-start.2 = ((f32[8,1,65536]{2,1,0:T(1,128)}), f32[8,1,65536]{2,1,0:T(1,128)}, u32[]{:S(2)}, u32[]{:S(2)}) async-start(f32[8,1,65536]{2,1,0:T(1,128)} %reshape.33), calls=%async_computation.2 | async-start | bytes 4194304 | tf_op jit(solution)/shard_map/all_to_all | solution.py:21
  180.9 66.5 %all-gather = f32[8,4,32]{2,1,0:T(4,128)S(1)} all-gather(f32[1,4,32]{2,1,0:T(4,128)S(1)} %bitcast.85), channel_id=1, replica_groups=mesh['row'=4,'col'=8] {'col'}, dimensions={0}, use_global_device_ids=true | all-gather | bytes 4608 | tf_op jit(solution)/shard_map/all_gather | solution.py:20
  247.3 7.2 %reduce.7 = f32[8,65536]{1,0:T(8,128)S(1)} reduce(f32[8,1,65536]{2,1,0:T(1,128)} %all-to-all-done.2, f32[]{:T(128)} %broadcast.53), dimensions={1}, to_apply=%all_to_all.58.reduce_sub_computation | reduce | bytes 4194308 | tf_op jit(solution)/shard_map/all_to_all | solution.py:21
  254.6 17.3 %reshape.34 = f32[1024,8,4,16]{3,2,1,0:T(4,128)} reshape(f32[8,65536]{1,0:T(8,128)S(1)} %reduce.7) | data formatting | bytes 4194304
  271.9 9.8 %copy.35 = f32[8,128,8,4,16]{1,0,4,3,2:T(8,128)S(1)} copy(f32[8,128,8,4,16]{4,3,2,1,0:T(4,128)} %bitcast.74) | data formatting | bytes 4194304 | tf_op jit(solution)/shard_map/all_to_all | solution.py:21
  281.7 1.4 copy.25
  283.1 1.9 convolution_bitcast_fusion
  285.0 1.2 copy.27
  286.2 46.2 %all_to_all.70 = f32[128,8,32,16]{0,3,1,2:T(8,128)S(1)} all-to-all(f32[128,8,32,16]{0,3,1,2:T(8,128)S(1)} %copy.27), channel_id=1, replica_groups=mesh['row'=4,'col'=8] {'col'}, dimensions={2} | all-to-all | bytes 4194304 | tf_op jit(solution)/shard_map/all_to_all | solution.py:23
  332.5 1.2 copy.28
  333.7 8.9 %fusion.14 = f32[1024,1024]{1,0:T(8,128)} fusion(f32[64,8,8,128]{3,2,1,0:T(8,128)S(1)} %bitcast.75), kind=kOutput, calls=%fused_computation.20 | convolution fusion | flops 6442450944 | bytes 6291456 | tf_op jit(solution)/shard_map/dot_general | solution.py:26
  342.7 1.9 copy.41
  344.5 138.8 %all-reduce.2.cloned.1.call-done = f32[1024,1024]{1,0:T(8,128)} async-done(((f32[1024,1024]{1,0:T(8,128)}), f32[1024,1024]{1,0:T(8,128)}) %all-reduce.2.cloned.1.call-update) | async-done | bytes 4194320 | tf_op jit(solution)/shard_map/psum | solution.py:27
  483.4 6.3 %fusion.15 = f32[1024,64]{0,1:T(8,128)S(1)} fusion(f32[1024,1024]{1,0:T(8,128)} %all-reduce.2.cloned.1.call-done, f32[1024,64]{0,1:T(8,128)S(1)} %copy-done), kind=kOutput, calls=%fused_computation.21 | convolution fusion | flops 805306368 | bytes 4718592 | tf_op jit(solution)/shard_map/dot_general | solution.py:28
  490.2 5.8 %cholesky.16 = f32[64,64]{1,0:T(8,128)S(1)} custom-call(f32[64,64]{1,0:T(8,128)S(1)} %fusion.10), custom_call_target="Cholesky" | custom-call | tf_op jit(solution)/shard_map/jit(cholesky)/cholesky | solution.py:30
  497.3 4.9 custom-call.7
  502.7 2.5 fusion.5
  (25 shorter events, 2.8 us)
Async XLA Ops:
  7.2 476.2 %copy-start = (f32[1024,64]{0,1:T(8,128)S(1)}, f32[1024,64]{0,1:T(8,128)}, u32[]{:S(2)}) copy-start(f32[1024,64]{0,1:T(8,128)} %param.9) | copy-start | bytes 786436
  7.2 5.5 %copy-start.4 = (f32[32,16]{0,1:T(8,128)S(1)}, f32[32,16]{0,1:T(8,128)}, u32[]{:S(2)}) copy-start(f32[32,16]{0,1:T(8,128)} %param.8) | copy-start | bytes 6148
  44.5 4.4 copy-start.5
  44.5 31.1 %all-to-all-start = ((f32[4,1,131072]{2,1,0:T(1,128)}), f32[4,1,131072]{2,1,0:T(1,128)S(1)}, u32[]{:S(2)}, u32[]{:S(2)}) async-start(f32[4,1,131072]{2,1,0:T(1,128)} %reshape.31), calls=%async_computation | async-start | bytes 4194304 | tf_op jit(solution)/shard_map/all_to_all | solution.py:17
  75.5 1.4 copy-start.2
  174.0 6.8 %copy-start.6 = (f32[4,32]{1,0:T(4,128)S(1)}, f32[4,32]{1,0:T(4,128)}, u32[]{:S(2)}) copy-start(f32[4,32]{1,0:T(4,128)} %param.7) | copy-start | bytes 1540
  174.0 73.3 %all-to-all-start.2 = ((f32[8,1,65536]{2,1,0:T(1,128)}), f32[8,1,65536]{2,1,0:T(1,128)}, u32[]{:S(2)}, u32[]{:S(2)}) async-start(f32[8,1,65536]{2,1,0:T(1,128)} %reshape.33), calls=%async_computation.2 | async-start | bytes 4194304 | tf_op jit(solution)/shard_map/all_to_all | solution.py:21
  180.8 302.5 %all-reduce.2.cloned.1.call-start = ((), (), s32[]{:S(2)}) async-start(), calls=%async_computation.4 | async-start | bytes 8388608 | tf_op jit(solution)/shard_map/psum | solution.py:27
  344.5 158.2 %copy-start.1 = (f32[64,8,8,128]{3,1,2,0:T(8,128)S(1)}, f32[64,8,8,128]{3,1,2,0:T(8,128)}, u32[]{:S(2)}) copy-start(f32[64,8,8,128]{3,1,2,0:T(8,128)} %copy.41) | copy-start | bytes 6291460
  502.7 2.5 copy-start.3
Sparse Core Ops, SparseCore 0:
  342.8 140.5 all-reduce.1
where the time goes:
time: 518 us; the launch traced here: 512 us
  blocking collectives  168 us (32%)
  waiting for transfers between devices  139 us (27%)
  local copies, waits for them, and re-layouts  127 us (25%)
  other arithmetic  27 us (5%)
  matrix products  26.5 us (5%)
  between operations  14.6 us (3%)
  starting transfers between devices  11.2 us (2%)
    psum x1, waiting for transfers between devices, shards(): gram = lax.psum(local_gram, ('row', 'col'))  139 us
    unnamed x20, local copies, waits for them, and re-layouts  74.8 us
    all_gather x1, blocking collectives, shards(): whole_three = lax.all_gather(factor_three, 'col', axis=0, tiled=True)  66.5 us
    all_to_all x1, blocking collectives, shards(): lax.all_to_all(projected_three, 'col', split_axis=2, concat_axis=0, tiled...  46.2 us
    all_to_all x1, blocking collectives, shards(): lax.all_to_all(projected_two, 'row', split_axis=1, concat_axis=0, tiled=T...  28.1 us
    all_gather x1, blocking collectives, shards(): whole_two = lax.all_gather(factor_two, 'row', axis=0, tiled=True)  26.7 us
    all_to_all x2, local copies, waits for them, and re-layouts, shards(): lax.all_to_all(fourth, 'row', split_axis=0, concat_axis=1, tiled=True)  12.7 us
    dot_general x1, local copies, waits for them, and re-layouts, shards(): fourth = jnp.einsum('abcd,de->abce', data, factor_four, precision=highest)  12.2 us
  transfers between devices with their start and end apart: 3, of which 1 were waited for; matrix products, arithmetic and copies ran while one was open for 0% of the time, Pallas kernels for 0%

commit v1 on v0

--- a/solution.py
+++ b/solution.py
@@ -2,6 +2,22 @@
 import jax.numpy as jnp
 from jax import lax
 from jax.sharding import PartitionSpec as P
+
+
+def pairwise_exchange(x, axis, split, join):
+    ways, here = (lax.axis_size(axis), lax.axis_index(axis))
+    width = x.shape[split] // ways
+    shape = list(x.shape)
+    shape[split] = width
+    height = shape[join]
+    shape[join] = height * ways
+    full = jnp.zeros(shape, x.dtype)
+    for mask in range(ways):
+        part = lax.dynamic_slice_in_dim(x, (here ^ mask) * width, width, axis=split)
+        if mask:
+            part = lax.ppermute(part, axis, [(d, d ^ mask) for d in range(ways)])
+        full = lax.dynamic_update_slice_in_dim(full, part, (here ^ mask) * height, axis=join)
+    return full
 
 
 def shards(tensor, factor_two, factor_three, factor_four, factor_init):
@@ -16,7 +32,7 @@
     whole_two = lax.all_gather(factor_two, "row", axis=0, tiled=True)
     spread_two = lax.all_to_all(fourth, "row", split_axis=0, concat_axis=1, tiled=True)
     projected_two = jnp.einsum("abce,bg->agce", spread_two, whole_two, precision=highest)
-    partial_two = lax.all_to_all(projected_two, "row", split_axis=1, concat_axis=0, tiled=True)
+    partial_two = pairwise_exchange(projected_two, "row", 1, 0)
     whole_three = lax.all_gather(factor_three, "col", axis=0, tiled=True)
     spread_three = lax.all_to_all(partial_two, "col", split_axis=0, concat_axis=2, tiled=True)
     projected_three = jnp.einsum("agce,cf->agfe", spread_three, whole_three, precision=highest)

time: 518 us -> 520 us (level)
  local copies, waits for them, and re-layouts: 127 us -> 154 us
  blocking collectives: 168 us -> 141 us
    all_to_all x1 -> x0, blocking collectives: 28.1 us -> none  [shards(): lax.all_to_all(projected_two, 'row', split_axis=1, concat_axis=0, tiled=T...]
    dynamic_update_slice x0 -> x4, local copies, waits for them, and re-layouts: none -> 16.2 us  [pairwise_exchange(): lax.dynamic_update_slice_in_dim(full, part, (here ^ mask) * height, axis=...]
    ppermute x0 -> x3, local copies, waits for them, and re-layouts: none -> 13.3 us  [pairwise_exchange(): part = lax.ppermute(part, axis, [(d, d ^ mask) for d in range(ways)])]
    all_to_all x1 -> x0, local copies, waits for them, and re-layouts: 12.1 us -> none  [shards(): lax.all_to_all(projected_two, 'row', split_axis=1, concat_axis=0, tiled=T...]
    broadcast_in_dim x0 -> x1, local copies, waits for them, and re-layouts: none -> 6.34 us  [pairwise_exchange(): full = jnp.zeros(shape, x.dtype)]
    unnamed x20 -> x24, local copies, waits for them, and re-layouts: 74.8 us -> 74.8 us
  transfers between devices with their start and end apart: 3 -> 6, of which waited for: 1 -> 1; matrix products, arithmetic and copies ran while one was open for 0% -> 6% of each run, Pallas kernels for 0% -> 0%
where the time goes in v1:
time: 520 us; the launch traced here: 515 us
  local copies, waits for them, and re-layouts  154 us (30%)
  blocking collectives  141 us (27%)
  waiting for transfers between devices  139 us (27%)
  other arithmetic  27 us (5%)
  matrix products  26.5 us (5%)
  between operations  14.6 us (3%)
  starting transfers between devices  13.1 us (3%)
    psum x1, waiting for transfers between devices, shards(): gram = lax.psum(local_gram, ('row', 'col'))  139 us
    unnamed x24, local copies, waits for them, and re-layouts  74.8 us
    all_gather x1, blocking collectives, shards(): whole_three = lax.all_gather(factor_three, 'col', axis=0, tiled=True)  67.6 us
    all_to_all x1, blocking collectives, shards(): lax.all_to_all(projected_three, 'col', split_axis=2, concat_axis=0, tiled...  46.3 us
    all_gather x1, blocking collectives, shards(): whole_two = lax.all_gather(factor_two, 'row', axis=0, tiled=True)  26.7 us
    dynamic_update_slice x4, local copies, waits for them, and re-layouts, pairwise_exchange(): lax.dynamic_update_slice_in_dim(full, part, (here ^ mask) * height, axis=...  16.2 us
    ppermute x3, local copies, waits for them, and re-layouts, pairwise_exchange(): part = lax.ppermute(part, axis, [(d, d ^ mask) for d in range(ways)])  13.3 us
    all_to_all x2, local copies, waits for them, and re-layouts, shards(): lax.all_to_all(fourth, 'row', split_axis=0, concat_axis=1, tiled=True)  12.7 us
  transfers between devices with their start and end apart: 6, of which 1 were waited for; matrix products, arithmetic and copies ran while one was open for 6% of the time, Pallas kernels for 0%

profile of v1, /device:TPU:0, one launch (start us, length us, event | category | flops | bytes accessed | tf_op | source)
XLA Modules:
  0.0 514.6 jit_solution(8935516204427921779)
XLA Ops:
  7.2 5.5 %copy.21 = f32[1024,8,128]{0,2,1:T(8,128)} copy(f32[1024,8,128]{2,1,0:T(8,128)} %param.5) | data formatting | bytes 8388608 | tf_op args[0]
  12.7 4.2 fusion.9
  16.8 12.1 %copy.22 = f32[1024,8,4,16]{3,2,1,0:T(4,128)} copy(f32[1024,8,4,16]{0,3,2,1:T(8,128)S(1)} %fusion.9) | data formatting | bytes 4194304 | tf_op jit(solution)/shard_map/abcd,de->abce/dot_general | solution.py:31
  28.9 15.5 %reshape.31 = f32[4,1,131072]{2,1,0:T(1,128)} reshape(f32[1024,8,4,16]{3,2,1,0:T(4,128)} %copy.22) | data formatting | bytes 4194304
  44.4 4.4 all-to-all-start
  48.8 26.7 %all_gather.6 = f32[32,32]{1,0:T(8,128)S(1)} all-gather(f32[8,32]{1,0:T(8,128)S(1)} %copy-done.7), channel_id=1, replica_groups=mesh['row'=4,'col'=8] {'row'}, dimensions={0}, use_global_device_ids=true | all-gather | bytes 5120 | tf_op jit(solution)/shard_map/all_gather | solution.py:32
  77.3 7.7 %reduce.6 = f32[4,131072]{1,0:T(4,128)S(1)} reduce(f32[4,1,131072]{2,1,0:T(1,128)} %copy-done.4, f32[]{:T(128)} %broadcast.53), dimensions={1}, to_apply=%all_to_all.37.reduce_sub_computation | reduce | bytes 4194308 | tf_op jit(solution)/shard_map/all_to_all | solution.py:33
  85.0 18.0 %reshape.32 = f32[1024,8,4,16]{3,2,1,0:T(4,128)} reshape(f32[4,131072]{1,0:T(4,128)S(1)} %reduce.6) | data formatting | bytes 4194304
  103.0 12.2 %copy.23 = f32[4,256,8,4,16]{1,2,0,4,3:T(8,128)S(1)} copy(f32[4,256,8,4,16]{4,3,2,1,0:T(4,128)} %bitcast.71) | data formatting | bytes 4194304 | tf_op jit(solution)/shard_map/all_to_all | solution.py:33
  118.2 4.4 copy.24
  123.7 6.3 %broadcast_in_dim.5 = f32[1024,8,4,16]{3,2,1,0:T(4,128)} broadcast(f32[]{:T(128)} %constant.52.clone.1), dimensions={} | broadcast | bytes 2097156 | tf_op jit(solution)/shard_map/broadcast_in_dim | solution.py:14
  130.1 2.9 constant_dynamic-update-slice_fusion.3
  133.0 4.4 copy.25
  137.3 4.4 copy.26
  141.7 5.3 %constant_dynamic-update-slice_fusion.2 = f32[1024,8,4,16]{3,2,1,0:T(4,128)} fusion(f32[1024,8,4,16]{3,2,1,0:T(4,128)} %constant_dynamic-update-slice_fusion.3, f32[256,8,4,16]{3,2,1,0:T(4,128)} %copy.25, s32[]{:T(128)S(6)} %select_n.31), kind=kLoop, calls=%fused_computation.24 | loop fusion | bytes 8388612 | tf_op jit(solution)/shard_map/dynamic_update_slice | solution.py:19
  147.0 2.9 constant_dynamic-update-slice_fusion.1
  149.9 4.5 copy.27
  154.5 5.1 constant_dynamic-update-slice_fusion
  159.6 15.4 %reshape.33 = f32[8,1,65536]{2,1,0:T(1,128)} reshape(f32[1024,8,4,16]{3,2,1,0:T(4,128)} %constant_dynamic-update-slice_fusion) | data formatting | bytes 4194304
  174.9 6.8 %all-to-all-start.1 = ((f32[8,1,65536]{2,1,0:T(1,128)}), f32[8,1,65536]{2,1,0:T(1,128)}, u32[]{:S(2)}, u32[]{:S(2)}) async-start(f32[8,1,65536]{2,1,0:T(1,128)} %reshape.33), calls=%async_computation.1 | async-start | bytes 4194304 | tf_op jit(solution)/shard_map/all_to_all | solution.py:37
  181.8 67.6 %all-gather = f32[8,4,32]{2,1,0:T(4,128)S(1)} all-gather(f32[1,4,32]{2,1,0:T(4,128)S(1)} %bitcast.82), channel_id=1, replica_groups=mesh['row'=4,'col'=8] {'col'}, dimensions={0}, use_global_device_ids=true | all-gather | bytes 4608 | tf_op jit(solution)/shard_map/all_gather | solution.py:36
  249.4 7.2 %reduce.7 = f32[8,65536]{1,0:T(8,128)S(1)} reduce(f32[8,1,65536]{2,1,0:T(1,128)} %all-to-all-done.1, f32[]{:T(128)} %broadcast.53), dimensions={1}, to_apply=%all_to_all.41.reduce_sub_computation | reduce | bytes 4194308 | tf_op jit(solution)/shard_map/all_to_all | solution.py:37
  256.6 17.3 %reshape.34 = f32[1024,8,4,16]{3,2,1,0:T(4,128)} reshape(f32[8,65536]{1,0:T(8,128)S(1)} %reduce.7) | data formatting | bytes 4194304
  273.9 9.8 %copy.38 = f32[8,128,8,4,16]{1,0,4,3,2:T(8,128)S(1)} copy(f32[8,128,8,4,16]{4,3,2,1,0:T(4,128)} %bitcast.72) | data formatting | bytes 4194304 | tf_op jit(solution)/shard_map/all_to_all | solution.py:37
  285.1 1.9 convolution_bitcast_fusion
  288.3 46.3 %all_to_all.51 = f32[128,8,32,16]{0,3,1,2:T(8,128)S(1)} all-to-all(f32[128,8,32,16]{0,3,1,2:T(8,128)S(1)} %copy.31), channel_id=1, replica_groups=mesh['row'=4,'col'=8] {'col'}, dimensions={2} | all-to-all | bytes 4194304 | tf_op jit(solution)/shard_map/all_to_all | solution.py:39
  335.8 8.9 %fusion.11 = f32[1024,1024]{1,0:T(8,128)} fusion(f32[64,8,8,128]{3,2,1,0:T(8,128)S(1)} %bitcast.73), kind=kOutput, calls=%fused_computation.27 | convolution fusion | flops 6442450944 | bytes 6291456 | tf_op jit(solution)/shard_map/dot_general | solution.py:42
  346.6 138.9 %all-reduce.2.cloned.1.call-done = f32[1024,1024]{1,0:T(8,128)} async-done(((f32[1024,1024]{1,0:T(8,128)}), f32[1024,1024]{1,0:T(8,128)}) %all-reduce.2.cloned.1.call-update) | async-done | bytes 4194320 | tf_op jit(solution)/shard_map/psum | solution.py:43
  485.5 6.3 %fusion.12 = f32[1024,64]{0,1:T(8,128)S(1)} fusion(f32[1024,1024]{1,0:T(8,128)} %all-reduce.2.cloned.1.call-done, f32[1024,64]{0,1:T(8,128)S(1)} %copy-done), kind=kOutput, calls=%fused_computation.28 | convolution fusion | flops 805306368 | bytes 4718592 | tf_op jit(solution)/shard_map/dot_general | solution.py:44
  492.3 5.8 %cholesky.16 = f32[64,64]{1,0:T(8,128)S(1)} custom-call(f32[64,64]{1,0:T(8,128)S(1)} %fusion.7), custom_call_target="Cholesky" | custom-call | tf_op jit(solution)/shard_map/jit(cholesky)/cholesky | solution.py:46
  499.5 4.9 custom-call.7
  504.9 2.5 fusion.2
  (42 shorter events, 13.9 us)
Async XLA Ops:
  7.2 478.4 %copy-start = (f32[1024,64]{0,1:T(8,128)S(1)}, f32[1024,64]{0,1:T(8,128)}, u32[]{:S(2)}) copy-start(f32[1024,64]{0,1:T(8,128)} %param.9) | copy-start | bytes 786436
  7.2 5.5 %copy-start.6 = (f32[32,16]{0,1:T(8,128)S(1)}, f32[32,16]{0,1:T(8,128)}, u32[]{:S(2)}) copy-start(f32[32,16]{0,1:T(8,128)} %param.8) | copy-start | bytes 6148
  44.4 4.4 copy-start.7
  44.4 31.1 %all-to-all-start = ((f32[4,1,131072]{2,1,0:T(1,128)}), f32[4,1,131072]{2,1,0:T(1,128)S(1)}, u32[]{:S(2)}, u32[]{:S(2)}) async-start(f32[4,1,131072]{2,1,0:T(1,128)} %reshape.31), calls=%async_computation | async-start | bytes 4194304 | tf_op jit(solution)/shard_map/all_to_all | solution.py:33
  75.5 1.3 copy-start.4
  117.4 15.5 %collective-permute-start = (f32[256,8,4,16]{0,1,3,2:T(8,128)S(1)}, f32[256,8,4,16]{0,1,3,2:T(8,128)S(1)}, u32[]{:S(2)}, u32[]{:S(2)}) collective-permute-start(f32[256,8,4,16]{0,1,3,2:T(8,128)S(1)} %get-tuple-element.4), channel_id=1, source_target_pairs={{0,8},{8,0},{16,24},{24,16},{1,9},{9,1},{17,25},{25,17},{2,10},{10... | collective-permute-start | bytes 1572872 | tf_op jit(solution)/shard_map/ppermute | solution.py:18
  117.8 19.5 %collective-permute-start.1 = (f32[256,8,4,16]{0,1,3,2:T(8,128)S(1)}, f32[256,8,4,16]{0,1,3,2:T(8,128)S(1)}, u32[]{:S(2)}, u32[]{:S(2)}) collective-permute-start(f32[256,8,4,16]{0,1,3,2:T(8,128)S(1)} %get-tuple-element.3), channel_id=1, source_target_pairs={{0,16},{8,24},{16,0},{24,8},{1,17},{9,25},{17,1},{25,9},{2,18},{10... | collective-permute-start | bytes 1572872 | tf_op jit(solution)/shard_map/ppermute | solution.py:18
  122.6 7.5 %copy-start.1 = (f32[256,8,4,16]{3,2,1,0:T(4,128)S(1)}, f32[256,8,4,16]{3,2,1,0:T(4,128)}, u32[]{:S(2)}) copy-start(f32[256,8,4,16]{3,2,1,0:T(4,128)} %copy.24) | copy-start | bytes 1572868
  122.6 27.4 %collective-permute-start.2 = (f32[256,8,4,16]{0,1,3,2:T(8,128)S(1)}, f32[256,8,4,16]{0,1,3,2:T(8,128)S(1)}, u32[]{:S(2)}, u32[]{:S(2)}) collective-permute-start(f32[256,8,4,16]{0,1,3,2:T(8,128)S(1)} %get-tuple-element.2), channel_id=1, source_target_pairs={{0,24},{8,16},{16,8},{24,0},{1,25},{9,17},{17,9},{25,1},{2,26},{10... | collective-permute-start | bytes 1572872 | tf_op jit(solution)/shard_map/ppermute | solution.py:18
  141.7 5.3 %copy-start.2 = (f32[256,8,4,16]{3,2,1,0:T(4,128)S(1)}, f32[256,8,4,16]{3,2,1,0:T(4,128)}, u32[]{:S(2)}) copy-start(f32[256,8,4,16]{3,2,1,0:T(4,128)} %copy.26) | copy-start | bytes 1572868
  174.9 6.8 %copy-start.8 = (f32[4,32]{1,0:T(4,128)S(1)}, f32[4,32]{1,0:T(4,128)}, u32[]{:S(2)}) copy-start(f32[4,32]{1,0:T(4,128)} %param.7) | copy-start | bytes 1540
  174.9 74.4 %all-to-all-start.1 = ((f32[8,1,65536]{2,1,0:T(1,128)}), f32[8,1,65536]{2,1,0:T(1,128)}, u32[]{:S(2)}, u32[]{:S(2)}) async-start(f32[8,1,65536]{2,1,0:T(1,128)} %reshape.33), calls=%async_computation.1 | async-start | bytes 4194304 | tf_op jit(solution)/shard_map/all_to_all | solution.py:37
  181.7 303.8 %all-reduce.2.cloned.1.call-start = ((), (), s32[]{:S(2)}) async-start(), calls=%async_computation.3 | async-start | bytes 8388608 | tf_op jit(solution)/shard_map/psum | solution.py:43
  346.6 158.3 %copy-start.3 = (f32[64,8,8,128]{3,1,2,0:T(8,128)S(1)}, f32[64,8,8,128]{3,1,2,0:T(8,128)}, u32[]{:S(2)}) copy-start(f32[64,8,8,128]{3,1,2,0:T(8,128)} %copy.43) | copy-start | bytes 6291460
  504.8 2.5 copy-start.5
Sparse Core Ops, SparseCore 0:
  344.9 140.6 all-reduce.1
